TPU v7x, 32 devices: a whole 2x2x4 slice. The times are simulated.
32 devices in a mesh: dp: 8 (over y, x, core), tensor: 4 (over z).
Axes of the slice: x: 2, y: 2, z: 4, core: 2. Of those that a mesh axis runs over, the one named last changes fastest.
Arguments:
- inputs: bfloat16 [2048, 2048], P('dp'), may hold values from -6 to 6
- ln_gain: float32 [2048], replicated, may hold values from 0.5 to 1.5
- ln_bias: float32 [2048], replicated, may hold values from -1.75 to 1.75
- w_qkv: bfloat16 [2048, 6144], P(None, 'tensor'), may hold values from -1 to 1
- b_qkv: float32 [6144], P('tensor'), may hold values from -1.75 to 1.75
- w_out: bfloat16 [2048, 2048], P('tensor'), may hold values from -0.75 to 0.75
- b_out: float32 [2048], replicated, may hold values from -1.75 to 1.75
- w_fc1: bfloat16 [2048, 8192], P(None, 'tensor'), may hold values from -0.125 to 0.125
- b_fc1: float32 [8192], P('tensor'), may hold values from -3 to 3
- w_fc2: bfloat16 [8192, 2048], P('tensor'), may hold values from -0.0625 to 0.0625
- b_fc2: float32 [2048], replicated, may hold values from -1.75 to 1.75
- cotangent: bfloat16 [2048, 2048], P('dp')
Outputs:
- output: bfloat16 [2048, 2048], P('dp')
- input_grad: float32 [2048, 2048], P('dp')
- grad_ln_gain: float32 [2048], replicated
- grad_ln_bias: float32 [2048], replicated
- grad_w_qkv: float32 [2048, 6144], P(None, 'tensor')
- grad_b_qkv: float32 [6144], P('tensor')
- grad_w_out: float32 [2048, 2048], P('tensor')
- grad_b_out: float32 [2048], replicated
- grad_w_fc1: float32 [2048, 8192], P(None, 'tensor')
- grad_b_fc1: float32 [8192], P('tensor')
- grad_w_fc2: float32 [8192, 2048], P('tensor')
- grad_b_fc2: float32 [2048], replicated
All inputs are finite; a program needn't handle non-finite values.
Results may differ from a plain program's by a relative error of at most 0.02.
Values may be sent and summed in bfloat16 or wider, within the bound.
A program may use at most 320 MiB of HBM per device.

v0:
```python
import jax
import jax.numpy as jnp
from jax import lax
from jax.sharding import PartitionSpec as P

HD = 64
ROT = 32
EPS = 1e-05
GELU_C = 0.7978845608028654
GELU_A = 0.044715


def gelu(argument):
    inner = GELU_C * (argument + GELU_A * argument * argument * argument)
    return 0.5 * argument * (1.0 + jnp.tanh(inner))


def gelu_slope(argument):
    tangent = jnp.tanh(GELU_C * (argument + GELU_A * argument * argument * argument))
    return 0.5 * (1.0 + tangent) + 0.5 * argument * (1.0 - tangent * tangent) * GELU_C * (
        1.0 + 3.0 * GELU_A * argument * argument
    )


def rotary_tables(length):
    position = jnp.arange(length).astype(jnp.float32)
    freqs = 10000.0 ** (-(jnp.arange(ROT // 2).astype(jnp.float32) * 2.0 / ROT))
    angles = position[:, None] * freqs[None, :]
    return (jnp.cos(angles)[:, None, :], jnp.sin(angles)[:, None, :])


def rotate(tensor, cosine, sine):
    first = tensor[..., : ROT // 2]
    second = tensor[..., ROT // 2 : ROT]
    return jnp.concatenate(
        [first * cosine - second * sine, second * cosine + first * sine, tensor[..., ROT:]], axis=-1
    )


def unrotate(grad, cosine, sine):
    first = grad[..., : ROT // 2]
    second = grad[..., ROT // 2 : ROT]
    return jnp.concatenate(
        [first * cosine + second * sine, second * cosine - first * sine, grad[..., ROT:]], axis=-1
    )


def probabilities(query_rot, key_rot, logsum):
    length = query_rot.shape[0]
    scores = jnp.einsum(
        "qhd,khd->hqk", query_rot, key_rot, preferred_element_type=jnp.float32
    ) * HD ** (-0.5)
    causal = jnp.arange(length)[:, None] >= jnp.arange(length)[None, :]
    scores = jnp.where(causal[None], scores, -1e30)
    top = jnp.max(scores, -1, keepdims=True)
    logsum = top + jnp.log(jnp.sum(jnp.exp(scores - top), -1, keepdims=True))
    return (jnp.exp(scores - logsum), logsum)


def per_device(
    inputs, ln_gain, ln_bias, w_qkv, b_qkv, w_out, b_out, w_fc1, b_fc1, w_fc2, b_fc2, cotangent
):
    length = inputs.shape[0]
    heads = w_out.shape[0] // HD
    cosine, sine = rotary_tables(length)
    widened = inputs.astype(jnp.float32)
    average = jnp.mean(widened, -1, keepdims=True)
    centered = widened - average
    inv_std = lax.rsqrt(jnp.mean(centered * centered, -1, keepdims=True) + EPS)
    normed_hat = centered * inv_std
    normed = (normed_hat * ln_gain + ln_bias).astype(jnp.bfloat16)
    projected = (jnp.dot(normed, w_qkv, preferred_element_type=jnp.float32) + b_qkv).reshape(
        length, heads, 3, HD
    )
    query_rot = rotate(projected[:, :, 0], cosine, sine).astype(jnp.bfloat16)
    key_rot = rotate(projected[:, :, 1], cosine, sine).astype(jnp.bfloat16)
    value_bf = projected[:, :, 2].astype(jnp.bfloat16)
    probs, logsum = probabilities(query_rot, key_rot, None)
    prob_bf = probs.astype(jnp.bfloat16)
    attended = jnp.einsum("hqk,khd->qhd", prob_bf, value_bf, preferred_element_type=jnp.float32)
    attended = attended.astype(jnp.bfloat16).reshape(length, heads * HD)
    hidden_pre = jnp.dot(normed, w_fc1, preferred_element_type=jnp.float32) + b_fc1
    activated = gelu(hidden_pre).astype(jnp.bfloat16)
    partial_value = jnp.dot(attended, w_out, preferred_element_type=jnp.float32) + jnp.dot(
        activated, w_fc2, preferred_element_type=jnp.float32
    )
    total = lax.psum(partial_value, "tensor")
    output = (widened + total + b_out + b_fc2).astype(jnp.bfloat16)
    g_bout = jnp.sum(cotangent.astype(jnp.float32), 0)
    g_w2 = jnp.dot(activated.T, cotangent, preferred_element_type=jnp.float32)
    dhidden = jnp.dot(cotangent, w_fc2.T, preferred_element_type=jnp.float32) * gelu_slope(
        hidden_pre
    )
    g_b1 = jnp.sum(dhidden, 0)
    dhidden_bf = dhidden.astype(jnp.bfloat16)
    g_w1 = jnp.dot(normed.T, dhidden_bf, preferred_element_type=jnp.float32)
    dnormed_local = jnp.dot(dhidden_bf, w_fc1.T, preferred_element_type=jnp.float32)
    g_wout = jnp.dot(attended.T, cotangent, preferred_element_type=jnp.float32)
    dattn_bf = (
        jnp.dot(cotangent, w_out.T, preferred_element_type=jnp.float32)
        .astype(jnp.bfloat16)
        .reshape(length, heads, HD)
    )
    delta = jnp.sum(
        dattn_bf.astype(jnp.float32) * attended.reshape(length, heads, HD).astype(jnp.float32), -1
    )
    dprob = jnp.einsum("qhd,khd->hqk", dattn_bf, value_bf, preferred_element_type=jnp.float32)
    dscore_bf = (probs * (dprob - jnp.transpose(delta)[:, :, None]) * HD ** (-0.5)).astype(
        jnp.bfloat16
    )
    dquery = jnp.einsum("hqk,khd->qhd", dscore_bf, key_rot, preferred_element_type=jnp.float32)
    dkey = jnp.einsum("hqk,qhd->khd", dscore_bf, query_rot, preferred_element_type=jnp.float32)
    dvalue = jnp.einsum("hqk,qhd->khd", prob_bf, dattn_bf, preferred_element_type=jnp.float32)
    dproj = jnp.stack(
        [unrotate(dquery, cosine, sine), unrotate(dkey, cosine, sine), dvalue], axis=2
    ).reshape(length, heads * 3 * HD)
    g_bqkv = jnp.sum(dproj, 0)
    dproj_bf = dproj.astype(jnp.bfloat16)
    g_wqkv = jnp.dot(normed.T, dproj_bf, preferred_element_type=jnp.float32)
    dnormed_local = dnormed_local + jnp.dot(dproj_bf, w_qkv.T, preferred_element_type=jnp.float32)
    dnormed = lax.psum(dnormed_local, "tensor")
    g_gain = jnp.sum(dnormed * normed_hat, 0)
    g_bias = jnp.sum(dnormed, 0)
    scaled = dnormed * ln_gain
    inner = (
        scaled
        - jnp.mean(scaled, -1, keepdims=True)
        - normed_hat * jnp.mean(scaled * normed_hat, -1, keepdims=True)
    )
    input_grad = cotangent.astype(jnp.float32) + inv_std * inner
    g_wqkv, g_bqkv, g_wout, g_bout, g_w1, g_b1, g_w2, g_gain, g_bias = lax.psum(
        (g_wqkv, g_bqkv, g_wout, g_bout, g_w1, g_b1, g_w2, g_gain, g_bias), "dp"
    )
    return (
        output,
        input_grad,
        g_gain,
        g_bias,
        g_wqkv,
        g_bqkv,
        g_wout,
        g_bout,
        g_w1,
        g_b1,
        g_w2,
        g_bout,
    )


def solution(mesh):
    placed = (
        P("dp", None),
        P(),
        P(),
        P(None, "tensor"),
        P("tensor"),
        P("tensor", None),
        P(),
        P(None, "tensor"),
        P("tensor"),
        P("tensor", None),
        P(),
        P("dp", None),
    )
    return jax.shard_map(
        per_device,
        mesh=mesh,
        in_specs=placed,
        out_specs=(
            P("dp", None),
            P("dp", None),
            P(),
            P(),
            P(None, "tensor"),
            P("tensor"),
            P("tensor", None),
            P(),
            P(None, "tensor"),
            P("tensor"),
            P("tensor", None),
            P(),
        ),
        check_vma=False,
    )
```

profile of v0, /device:TPU:0, one launch (start us, length us, event | category | flops | bytes accessed | tf_op | source)
XLA Modules:
  0.0 837.1 jit_solution(13396688774100656092)
XLA Ops:
  8.9 1.6 fusion.12
  13.2 5.8 convolution_add_fusion.1
  19.0 3.0 copy.44
  27.6 1.8 slice-done.9
  29.4 2.5 convolution_add_fusion.3
  32.0 2.6 fusion.36
  34.7 3.7 fusion.44
  39.6 5.0 fusion.45
  44.7 2.1 convolution_add_fusion
  46.8 3.7 convolution_add_fusion.2
  51.7 2.7 fusion.46
  54.5 6.9 fusion.38
  61.4 8.7 %fusion.24 = f32[2048,2048]{1,0:T(8,128)} fusion(bf16[256,2048]{1,0:T(8,128)(2,1)S(1)} %copy-done.22, bf16[256,2048]{1,0:T(8,128)(2,1)S(1)} %copy-done.2, f32[2048]{0:T(1024)S(1)} %copy-done.24, f32[2048]{0:T(1024)S(1)} %copy-done.23, f32[256]{0:T(256)S(1)} %add_rsqrt_fusion, f32[256]{0:T(256)S(1)} %broadcast_multiply_fusion.2), kind=kOutput, calls=%fused_computation.54 | convolution fusion | flops 2150629376 | bytes 18892800 | tf_op jit(solution)/shard_map/dot_general | solution.py:96
  70.1 8.8 %fusion.35 = f32[2048,2048]{1,0:T(8,128)} fusion(bf16[256,2048]{1,0:T(8,128)(2,1)S(1)} %copy-done.5, f32[256,2048]{1,0:T(8,128)S(1)} %copy-done.18), kind=kOutput, calls=%fused_computation.83 | convolution fusion | flops 2152202240 | bytes 19922944 | tf_op jit(solution)/shard_map/dot_general | solution.py:90
  81.6 126.8 %all-reduce.8.cloned.1.call-done = (f32[256,2048]{1,0:T(8,128)}, f32[256,2048]{1,0:T(8,128)}) async-done(((f32[256,2048]{1,0:T(8,128)}, f32[256,2048]{1,0:T(8,128)}), (f32[256,2048]{1,0:T(8,128)}, f32[256,2048]{1,0:T(8,128)})) %all-reduce.8.cloned.1.call-update) | async-done | bytes 4194320 | tf_op jit(solution)/shard_map/psum | solution.py:87
  208.4 2.7 fusion.11
  211.1 4.8 convert_reduce_fusion.1
  215.9 27.2 %all-reduce = (f32[2048]{0:T(1024)}, f32[2048]{0:T(1024)}, f32[1536]{0:T(1024)}, f32[2048]{0:T(1024)S(1)}, f32[2048]{0:T(1024)}) all-reduce(f32[2048]{0:T(1024)S(1)} %get-tuple-element.12, f32[2048]{0:T(1024)S(1)} %get-tuple-element.15, f32[1536]{0:T(1024)S(1)} %reduce_sum.110, ...), channel_id=1, replica_groups=mesh['dp'=8,'tensor'=4] {'dp'}, use_global_device_ids=true, to_apply=%region_10.11 | all-reduce | flops 9728 | bytes 77824 | tf_op jit(solution)/shard_map/psum | solution.py:131
  243.1 549.5 %all-reduce.6.cloned.1.call-done = (f32[2048,1536]{1,0:T(8,128)}, f32[512,2048]{1,0:T(8,128)}, f32[2048,2048]{1,0:T(8,128)}, f32[2048,2048]{1,0:T(8,128)}) async-done(((f32[2048,1536]{1,0:T(8,128)}, f32[512,2048]{1,0:T(8,128)}, f32[2048,2048]{1,0:T(8,128)}, f32[2048,2048]{1,0:T(8,128)}), (f32[2048,1536]{1,0:T(8,128)}, f32[512,2048]{1,0:T(8,128)}, f32[2048,2048]{1,0:T(8,128)}, ...) | async-done | bytes 50331664 | tf_op jit(solution)/shard_map/psum | solution.py:131
  793.2 10.6 %copy.81 = f32[2048,1536]{1,0:T(8,128)} copy(f32[2048,1536]{1,0:T(8,128)} %get-tuple-element.84) | data formatting | bytes 25165824
  803.8 4.8 copy.82
  808.7 13.6 %copy.83 = f32[2048,2048]{1,0:T(8,128)} copy(f32[2048,2048]{1,0:T(8,128)} %get-tuple-element.88) | data formatting | bytes 33554432
  822.2 1.7 slice-done.3
  824.0 6.3 copy.84
  (123 shorter events, 15.5 us)
Async XLA Ops:
  7.2 201.2 %all-reduce.8.cloned.1.call-start = ((), (), s32[]{:S(2)}) async-start(), calls=%async_computation.1 | async-start | bytes 8388608 | tf_op jit(solution)/shard_map/psum | solution.py:87
  25.6 19.1 %copy-start.13 = (bf16[8,64,256]{2,1,0:T(8,128)(2,1)}, bf16[8,64,256]{2,1,0:T(8,128)(2,1)S(1)}, u32[]{:S(2)}) copy-start(bf16[8,64,256]{2,1,0:T(8,128)(2,1)S(1)} %get-tuple-element.49) | copy-start | bytes 786436
  26.1 12.4 %copy-start.12 = (f32[256,8,1,64]{0,3,1,2:T(8,128)}, f32[256,8,1,64]{0,3,1,2:T(8,128)S(1)}, u32[]{:S(2)}) copy-start(f32[256,8,1,64]{0,3,1,2:T(8,128)S(1)} %convolution_bitcast_fusion) | copy-start | bytes 1572868
  27.2 4.7 copy-start.19
  27.5 4.4 copy-start.20
  27.5 4.4 slice-start.6
  34.6 3.7 slice-start.4
  34.6 3.8 slice-start.5
  38.3 8.5 %copy-start.21 = (bf16[256,2048]{1,0:T(8,128)(2,1)}, bf16[256,2048]{1,0:T(8,128)(2,1)S(1)}, u32[]{:S(2)}) copy-start(bf16[256,2048]{1,0:T(8,128)(2,1)S(1)} %get-tuple-element.51) | copy-start | bytes 3145732
  39.4 7.4 slice-start.10
  39.6 5.1 copy-start.15
  39.6 7.2 slice-start.11
  50.5 4.0 copy-start.16
  50.5 742.1 %all-reduce.6.cloned.1.call-start = ((), (), s32[]{:S(2)}) async-start(), calls=%async_computation | async-start | bytes 100663296 | tf_op jit(solution)/shard_map/psum | solution.py:131
  54.5 6.9 copy-start.22
  61.4 8.7 %copy-start.18 = (f32[256,2048]{1,0:T(8,128)S(1)}, f32[256,2048]{1,0:T(8,128)}, u32[]{:S(2)}) copy-start(f32[256,2048]{1,0:T(8,128)} %copy-done.17) | copy-start | bytes 6291460
  80.1 131.0 %copy-start.26 = (f32[2048]{0:T(1024)S(1)}, f32[2048]{0:T(1024)}, u32[]{:S(2)}) copy-start(f32[2048]{0:T(1024)} %param.22) | copy-start | bytes 24580
  80.1 131.0 %copy-start.27 = (f32[2048]{0:T(1024)S(1)}, f32[2048]{0:T(1024)}, u32[]{:S(2)}) copy-start(f32[2048]{0:T(1024)} %param.18) | copy-start | bytes 24580
  243.1 560.7 %copy-start.25 = (f32[2048]{0:T(1024)}, f32[2048]{0:T(1024)S(1)}, u32[]{:S(2)}) copy-start(f32[2048]{0:T(1024)S(1)} %get-tuple-element.87) | copy-start | bytes 24580
  803.8 18.4 %slice-start = ((s8[16777216]{0:T(1024)(128)(4,1)}), s8[4194304]{0:T(1024)(128)(4,1)S(1)}, s32[]{:S(2)}) async-start(s8[16777216]{0:T(1024)(128)(4,1)} %bitcast.53), calls=%async_computation.2 | async-start | bytes 8388608
  808.7 13.6 %slice-start.1 = ((s8[16777216]{0:T(1024)(128)(4,1)}), s8[4194304]{0:T(1024)(128)(4,1)S(1)}, s32[]{:S(2)}) async-start(s8[16777216]{0:T(1024)(128)(4,1)} %bitcast.53), calls=%async_computation.3 | async-start | bytes 8388608
  808.7 13.6 %slice-start.2 = ((s8[16777216]{0:T(1024)(128)(4,1)}), s8[4194304]{0:T(1024)(128)(4,1)S(1)}, s32[]{:S(2)}) async-start(s8[16777216]{0:T(1024)(128)(4,1)} %bitcast.53), calls=%async_computation.4 | async-start | bytes 8388608
  808.7 15.3 %slice-start.3 = ((s8[16777216]{0:T(1024)(128)(4,1)}), s8[4194304]{0:T(1024)(128)(4,1)S(1)}, s32[]{:S(2)}) async-start(s8[16777216]{0:T(1024)(128)(4,1)} %bitcast.53), calls=%async_computation.5 | async-start | bytes 8388608
  824.0 6.3 copy-start.1
  (20 other events, 44.0 us)
Sparse Core Ops, SparseCore 0:
  50.6 157.7 all-reduce.7
  213.8 578.7 all-reduce.5
where the time goes:
time: 838 us; the launch traced here: 837 us
  waiting for transfers between devices  676 us (81%)
  matrix products  56.8 us (7%)
  local copies, waits for them, and re-layouts  49.1 us (6%)
  blocking collectives  27.2 us (3%)
  between operations  14.7 us (2%)
  other arithmetic  13 us (2%)
    psum x1, waiting for transfers between devices, per_device(): lax.psum((g_wqkv, g_bqkv, g_wout, g_bout, g_w1, g_b1, g_w2, g_gain, g_bia...  549 us
    psum x1, waiting for transfers between devices, per_device(): total = lax.psum(partial_value, 'tensor')  127 us
    unnamed x85, local copies, waits for them, and re-layouts  43.4 us
    psum x1, blocking collectives, per_device(): lax.psum((g_wqkv, g_bqkv, g_wout, g_bout, g_w1, g_b1, g_w2, g_gain, g_bia...  27.2 us
  transfers between devices with their start and end apart: 2, of which 2 were waited for; matrix products, arithmetic and copies ran while one was open for 4% of the time, Pallas kernels for 0%

commit v1 on v0

--- a/solution.py
+++ b/solution.py
@@ -84,7 +84,8 @@
     partial_value = jnp.dot(attended, w_out, preferred_element_type=jnp.float32) + jnp.dot(
         activated, w_fc2, preferred_element_type=jnp.float32
     )
-    total = lax.psum(partial_value, "tensor")
+    parts = lax.all_gather(partial_value, "tensor", axis=0, tiled=False)
+    total = parts.sum(axis=0)
     output = (widened + total + b_out + b_fc2).astype(jnp.bfloat16)
     g_bout = jnp.sum(cotangent.astype(jnp.float32), 0)
     g_w2 = jnp.dot(activated.T, cotangent, preferred_element_type=jnp.float32)

time: 838 us -> 916 us (1.093)
  waiting for transfers between devices: 676 us -> 742 us
    all_gather x0 -> x1, waiting for transfers between devices: none -> 148 us  [per_device(): parts = lax.all_gather(partial_value, 'tensor', axis=0, tiled=False)]
    psum x1, waiting for transfers between devices: 127 us -> 49.4 us  [per_device(): dnormed = lax.psum(dnormed_local, 'tensor')]
    unnamed x85 -> x73, local copies, waits for them, and re-layouts: 43.4 us -> 44.8 us
  transfers between devices with their start and end apart: 2 -> 3, of which waited for: 2 -> 3; matrix products, arithmetic and copies ran while one was open for 4% -> 6% of each run, Pallas kernels for 0% -> 0%
where the time goes in v1:
time: 916 us
  waiting for transfers between devices  742 us (81%)
  matrix products  64.9 us (7%)
  local copies, waits for them, and re-layouts  50.6 us (6%)
  blocking collectives  27.5 us (3%)
  other arithmetic  16.4 us (2%)
  between operations  14.2 us (2%)
    psum x1, waiting for transfers between devices, per_device(): lax.psum((g_wqkv, g_bqkv, g_wout, g_bout, g_w1, g_b1, g_w2, g_gain, g_bia...  545 us
    all_gather x1, waiting for transfers between devices, per_device(): parts = lax.all_gather(partial_value, 'tensor', axis=0, tiled=False)  148 us
    psum x1, waiting for transfers between devices, per_device(): dnormed = lax.psum(dnormed_local, 'tensor')  49.4 us
    unnamed x73, local copies, waits for them, and re-layouts  44.8 us
    psum x1, blocking collectives, per_device(): lax.psum((g_wqkv, g_bqkv, g_wout, g_bout, g_w1, g_b1, g_w2, g_gain, g_bia...  27.5 us
  transfers between devices with their start and end apart: 3, of which 3 were waited for; matrix products, arithmetic and copies ran while one was open for 6% of the time, Pallas kernels for 0%

profile of v1, /device:TPU:0, one launch (start us, length us, event | category | flops | bytes accessed | tf_op | source)
XLA Modules:
  0.0 915.9 jit_solution(17900054274490643689)
XLA Ops:
  8.8 2.8 convolution_convert_fusion
  13.4 5.8 convolution_add_fusion.1
  19.2 3.0 copy.44
  30.6 3.2 fusion.45
  33.8 2.5 convolution_add_fusion.3
  36.3 7.8 fusion.44
  45.1 3.7 convolution_add_fusion.2
  48.9 6.6 fusion.36
  55.5 2.1 convolution_add_fusion
  58.8 2.7 fusion.46
  61.5 6.8 fusion.38
  68.3 8.7 fusion.24
  77.0 8.8 fusion.35
  88.4 49.4 %all-reduce.5.cloned.1.call-done = f32[256,2048]{1,0:T(8,128)} async-done(((f32[256,2048]{1,0:T(8,128)}), f32[256,2048]{1,0:T(8,128)}) %all-reduce.5.cloned.1.call-update) | async-done | bytes 2097168 | tf_op jit(solution)/shard_map/psum | solution.py:122
  137.8 2.6 fusion.11
  140.4 147.7 %all-gather.3.cloned.1.call-done = f32[1024,2048]{1,0:T(8,128)} async-done(((f32[256,2048]{1,0:T(8,128)}), f32[1024,2048]{1,0:T(8,128)}) %all-gather.3.cloned.1.call-update) | async-done | bytes 8388624 | tf_op jit(solution)/shard_map/all_gather | solution.py:87
  288.1 5.7 reduce_sum.113
  293.8 5.4 convert_reduce_fusion.1
  299.2 27.5 %all-reduce = (f32[2048]{0:T(1024)}, f32[2048]{0:T(1024)}, f32[1536]{0:T(1024)}, f32[2048]{0:T(1024)S(1)}, f32[2048]{0:T(1024)}) all-reduce(f32[2048]{0:T(1024)S(1)} %get-tuple-element.12, f32[2048]{0:T(1024)S(1)} %get-tuple-element.15, f32[1536]{0:T(1024)S(1)} %reduce_sum.120, ...), channel_id=1, replica_groups=mesh['dp'=8,'tensor'=4] {'dp'}, use_global_device_ids=true, to_apply=%region_10.11 | all-reduce | flops 9728 | bytes 77824 | tf_op jit(solution)/shard_map/psum | solution.py:132
  326.6 545.0 %all-reduce.7.cloned.1.call-done = (f32[2048,1536]{1,0:T(8,128)}, f32[512,2048]{1,0:T(8,128)}, f32[2048,2048]{1,0:T(8,128)}, f32[2048,2048]{1,0:T(8,128)}) async-done(((f32[2048,1536]{1,0:T(8,128)}, f32[512,2048]{1,0:T(8,128)}, f32[2048,2048]{1,0:T(8,128)}, f32[2048,2048]{1,0:T(8,128)}), (f32[2048,1536]{1,0:T(8,128)}, f32[512,2048]{1,0:T(8,128)}, f32[2048,2048]{1,0:T(8,128)}, ...) | async-done | bytes 50331664 | tf_op jit(solution)/shard_map/psum | solution.py:132
  872.3 10.6 %copy.80 = f32[2048,1536]{1,0:T(8,128)} copy(f32[2048,1536]{1,0:T(8,128)} %get-tuple-element.82) | data formatting | bytes 25165824
  882.9 4.8 copy.81
  887.7 13.6 %copy.82 = f32[2048,2048]{1,0:T(8,128)} copy(f32[2048,2048]{1,0:T(8,128)} %get-tuple-element.86) | data formatting | bytes 33554432
  903.1 6.3 copy.83
  (112 shorter events, 18.8 us)
Async XLA Ops:
  7.2 130.6 %all-reduce.5.cloned.1.call-start = ((), (), s32[]{:S(2)}) async-start(), calls=%async_computation | async-start | bytes 4194304 | tf_op jit(solution)/shard_map/psum | solution.py:122
  8.8 3.9 copy-start.2
  26.9 2.7 slice-start.6
  28.6 5.2 slice-start.4
  29.7 4.1 copy-start.12
  30.6 3.2 slice-start.5
  30.6 3.2 copy-start.24
  33.8 2.5 copy-start.3
  36.3 7.8 copy-start.14
  36.3 8.8 copy-start.25
  48.8 6.7 copy-start.11
  48.8 239.3 %all-gather.3.cloned.1.call-start = ((), (), s32[]{:S(2)}) async-start(), calls=%async_computation.1 | async-start | bytes 10485760 | tf_op jit(solution)/shard_map/all_gather | solution.py:87
  57.6 3.9 copy-start.13
  57.6 814.1 %all-reduce.7.cloned.1.call-start = ((), (), s32[]{:S(2)}) async-start(), calls=%async_computation.2 | async-start | bytes 100663296 | tf_op jit(solution)/shard_map/psum | solution.py:132
  61.5 6.8 copy-start.17
  68.3 8.7 copy-start.15
  288.1 5.7 copy-start.21
  288.1 5.7 copy-start.22
  326.6 556.2 %copy-start.20 = (f32[2048]{0:T(1024)}, f32[2048]{0:T(1024)S(1)}, u32[]{:S(2)}) copy-start(f32[2048]{0:T(1024)S(1)} %get-tuple-element.85) | copy-start | bytes 24580
  882.9 18.4 %slice-start = ((s8[16777216]{0:T(1024)(128)(4,1)}), s8[4194304]{0:T(1024)(128)(4,1)S(1)}, s32[]{:S(2)}) async-start(s8[16777216]{0:T(1024)(128)(4,1)} %bitcast.54), calls=%async_computation.3 | async-start | bytes 8388608
  887.7 13.6 %slice-start.1 = ((s8[16777216]{0:T(1024)(128)(4,1)}), s8[4194304]{0:T(1024)(128)(4,1)S(1)}, s32[]{:S(2)}) async-start(s8[16777216]{0:T(1024)(128)(4,1)} %bitcast.54), calls=%async_computation.4 | async-start | bytes 8388608
  887.7 13.6 %slice-start.2 = ((s8[16777216]{0:T(1024)(128)(4,1)}), s8[4194304]{0:T(1024)(128)(4,1)S(1)}, s32[]{:S(2)}) async-start(s8[16777216]{0:T(1024)(128)(4,1)} %bitcast.54), calls=%async_computation.5 | async-start | bytes 8388608
  887.7 15.3 %slice-start.3 = ((s8[16777216]{0:T(1024)(128)(4,1)}), s8[4194304]{0:T(1024)(128)(4,1)S(1)}, s32[]{:S(2)}) async-start(s8[16777216]{0:T(1024)(128)(4,1)} %bitcast.54), calls=%async_computation.6 | async-start | bytes 8388608
  903.1 6.3 copy-start.1
  (13 other events, 18.8 us)
Sparse Core Ops, SparseCore 0:
  48.9 88.8 all-reduce.4
  139.4 148.6 all-gather.2
  293.5 578.1 all-reduce.6
